TPU v7x, 256 devices: a whole 4x4x8 slice. The times are simulated.
256 devices in a mesh: inst: 4 (over y_hi, core), cells: 64 (over y_lo, x, z).
Axes of the slice: x: 4, y: 4 (y_hi: 2, y_lo: 2; y = y_hi * 2 + y_lo), z: 8, core: 2. Of those that a mesh axis runs over, the one named last changes fastest.
Arguments:
- flow_state: float32 [8, 5, 512, 32, 128], P('inst', None, 'cells'), may hold values from -6 to 6
- forcing: float32 [8, 5, 512, 32, 128], P('inst', None, 'cells'), may hold values from -6 to 6
- diffusion: float32 [512, 32, 128], P('cells'), may hold values from 0.2 to 0.6
- block_inverse: float32 [5, 5, 512, 32, 128], P(None, None, 'cells', 'inst'), may hold values from -0.03 to 0.15, as said below
Outputs:
- new_state: float32 [8, 5, 512, 32, 128], P('inst', None, 'cells')
Inputs may be any that keep to these rules, and one draw needn't show every extreme that they name: block_inverse[v, v] lies between 0.06 and 0.15; entries off the diagonal lie between -0.03 and 0.03.
All inputs are finite; a program needn't handle non-finite values.
Results may differ from a plain program's by a relative error of at most 0.0001.
Values sent between devices are 32-bit elements; how exact they have to be, the bound alone decides.
No kernel may reach another device: no remote copies, remote signals or barrier semaphores. Data moves between devices by JAX's collectives and lax.ppermute only.
A program may use at most 64 MiB of HBM per device.

v0:
```python
import math

import jax
import jax.numpy as jnp
from jax import lax
from jax.sharding import PartitionSpec as P

SWEEPS = 4


frequency = 1.0


def extended(shard, sides, width):
    edges = {}
    for axis, dim in sides:
        size, length = (lax.axis_size(axis), shard.shape[dim])
        up = [(i, (i + 1) % size) for i in range(size - 1)]
        last = lax.slice_in_dim(shard, length - width, length, axis=dim)
        initial = lax.slice_in_dim(shard, 0, width, axis=dim)
        edges[dim] = (
            lax.ppermute(last, axis, up),
            lax.ppermute(initial, axis, [(b, a) for a, b in up]),
        )
    done = []
    for _, dim in sides:
        low, high = edges[dim]
        around = [(width, width) if d in done else (0, 0) for d in range(shard.ndim)]
        shard = jnp.concatenate([jnp.pad(low, around), shard, jnp.pad(high, around)], axis=dim)
        done.append(dim)
    return shard


def extended_2(shard, sides, width):
    for axis, dim in sides:
        size, length = (lax.axis_size(axis), shard.shape[dim])
        up = [(i, (i + 1) % size) for i in range(size - 1)]
        down = [(j, i) for i, j in up]
        last = lax.slice_in_dim(shard, length - width, length, axis=dim)
        initial = lax.slice_in_dim(shard, 0, width, axis=dim)
        before = lax.ppermute(last, axis, up)
        after = lax.ppermute(initial, axis, down)
        shard = jnp.concatenate([before, shard, after], axis=dim)
    return shard


def spectral_matrix(count):
    index = jnp.arange(count)
    offset = index[:, None] - index[None, :]
    parity = jnp.where(offset % 2 == 0, 1.0, -1.0)
    angle = math.pi * jnp.where(offset == 0, 1, offset) / count
    entries = 0.5 * parity / jnp.tan(angle)
    return jnp.where(offset == 0, 0.0, entries).astype(jnp.float32)


def interior_sum(padded):
    padded = jnp.pad(padded, ((0, 0), (0, 0), (0, 0), (0, 0), (1, 1)))
    beside = padded[:, :, 2:, 1:-1, 1:-1] + padded[:, :, :-2, 1:-1, 1:-1]
    beside = beside + padded[:, :, 1:-1, 2:, 1:-1] + padded[:, :, 1:-1, :-2, 1:-1]
    beside = beside + padded[:, :, 1:-1, 1:-1, 2:] + padded[:, :, 1:-1, 1:-1, :-2]
    return beside


def block_neighbours(grid_field):
    padded = extended(grid_field, (("inst", 3), ("cells", 2)), 1)
    return interior_sum(padded)


def spectral_term(matrix, grid_field):
    flat = grid_field.reshape(grid_field.shape[0], -1)
    product = jnp.dot(matrix, flat, precision=lax.Precision.HIGHEST)
    return (frequency * product).reshape(grid_field.shape)


def apply_blocks(block_inverse, source):
    outputs = []
    for row_index in range(block_inverse.shape[0]):
        total = block_inverse[row_index, 0][None] * source[:, 0]
        for col_index in range(1, block_inverse.shape[1]):
            total = total + block_inverse[row_index, col_index][None] * source[:, col_index]
        outputs.append(total)
    return jnp.stack(outputs, axis=1)


def on_device(flow_state, forcing, diffusion, block_inverse):
    block_rows = block_inverse.shape[3]
    first_row = lax.axis_index("inst") * block_rows
    weight_block = lax.dynamic_slice_in_dim(diffusion, first_row, block_rows, 1)[None, None]
    matrix = spectral_matrix(lax.axis_size("inst") * flow_state.shape[0])
    padded = extended_2(flow_state, (("cells", 2),), 1)
    padded = jnp.pad(padded, ((0, 0), (0, 0), (0, 0), (1, 1), (0, 0)))
    local_part = diffusion[None, None] * (6.0 * flow_state - interior_sum(padded)) - forcing
    moved_state, moved_part = (
        lax.all_to_all(flow_state, "inst", split_axis=3, concat_axis=0, tiled=True),
        lax.all_to_all(local_part, "inst", split_axis=3, concat_axis=0, tiled=True),
    )
    residual = moved_part + spectral_term(matrix, moved_state)
    update = apply_blocks(block_inverse, -residual)
    for sweep_index in range(SWEEPS):
        source = -residual - spectral_term(matrix, update) + weight_block * block_neighbours(update)
        update = apply_blocks(block_inverse, source)
    return lax.all_to_all(moved_state + update, "inst", split_axis=0, concat_axis=3, tiled=True)


def solution(mesh):
    in_specs = (
        P("inst", None, "cells", None, None),
        P("inst", None, "cells", None, None),
        P("cells", None, None),
        P(None, None, "cells", "inst", None),
    )
    out_specs = P("inst", None, "cells", None, None)
    return jax.shard_map(
        on_device, mesh=mesh, in_specs=in_specs, out_specs=out_specs, check_vma=False
    )
```

profile of v0, /device:TPU:8, one launch (start us, length us, event | category | flops | bytes accessed | tf_op | source)
XLA Modules:
  0.0 190.7 jit_solution(16845610435672489864)
XLA Ops:
  0.0 3.1 %copy.21 = f32[2,5,8,32,128]{4,2,1,0,3:T(8,128)} copy(f32[2,5,8,32,128]{4,3,2,1,0:T(8,128)} %param.4) | data formatting | bytes 2621440 | tf_op args[0]
  3.1 3.7 %all-to-all-start = ((f32[2,5,8,32,128]{4,2,1,0,3:T(8,128)}), f32[2,5,8,32,128]{4,2,1,0,3:T(8,128)S(1)}, u32[]{:S(2)}, u32[]{:S(2)}) async-start(f32[2,5,8,32,128]{4,2,1,0,3:T(8,128)} %copy.21), calls=%async_computation | async-start | bytes 2621440 | tf_op jit(solution)/shard_map/all_to_all | solution.py:94
  6.8 1.0 fusion.144
  7.9 3.8 %collective-permute-start.1 = (f32[2,5,1,32,128]{4,3,2,1,0:T(8,128)S(1)}, f32[2,5,1,32,128]{4,3,2,1,0:T(8,128)S(1)}, u32[]{:S(2)}, u32[]{:S(2)}) collective-permute-start(f32[2,5,1,32,128]{4,3,2,1,0:T(8,128)S(1)} %get-tuple-element.21), channel_id=1, source_target_pairs={{0,1},{1,2},{2,3},{3,4},{4,5},{5,6},{6,7},{7,8},{8,9},{9,10},{10,1... | collective-permute-start | bytes 491528 | tf_op jit(solution)/shard_map/ppermute | solution.py:41
  11.7 8.8 %collective-permute-start = (f32[2,5,1,32,128]{4,3,2,1,0:T(8,128)S(1)}, f32[2,5,1,32,128]{4,3,2,1,0:T(8,128)S(1)}, u32[]{:S(2)}, u32[]{:S(2)}) collective-permute-start(f32[2,5,1,32,128]{4,3,2,1,0:T(8,128)S(1)} %get-tuple-element.22), channel_id=1, source_target_pairs={{1,0},{2,1},{3,2},{4,3},{5,4},{6,5},{7,6},{8,7},{9,8},{10,9},{11,1... | collective-permute-start | bytes 491528 | tf_op jit(solution)/shard_map/ppermute | solution.py:42
  20.6 2.9 %collective-permute-done.1 = f32[2,5,1,32,128]{4,3,2,1,0:T(8,128)S(1)} collective-permute-done((f32[2,5,1,32,128]{4,3,2,1,0:T(8,128)S(1)}, f32[2,5,1,32,128]{4,3,2,1,0:T(8,128)S(1)}, u32[]{:S(2)}, u32[]{:S(2)}) %collective-permute-start.1) | collective-permute-done | bytes 163872 | tf_op jit(solution)/shard_map/ppermute | solution.py:41
  23.7 0.9 collective-permute-done
  24.8 1.9 select_maximum_fusion.16
  26.7 5.4 %fusion.7 = f32[2,5,8,32,128]{4,2,1,0,3:T(8,128)} fusion(f32[2,5,10,34,128]{4,2,1,0,3:T(8,128)S(1)} %select_maximum_fusion.16, f32[2,5,8,32,128]{4,2,1,0,3:T(8,128)} %copy.21, f32[2,5,1,32,128]{4,2,1,0,3:T(1,128)S(1)} %copy.27, f32[2,5,1,32,128]{4,2,1,0,3:T(1,128)S(1)} %copy.26, f32[2,5,8,32,128]{4,3,2,1,0:T(8,128)S(1)} %copy-done.2, f32[8,32,128]{2,0,1:T(8,128)S(1)} %copy.23), kind=kLoop, calls=%fused_computation.36 | loop fusion | flops 3604480 | bytes 9797632 | tf_op jit(solution)/shard_map/sub | solution.py:92
  32.2 4.4 %all-to-all-start.1 = ((f32[2,5,8,32,128]{4,2,1,0,3:T(8,128)}), f32[2,5,8,32,128]{4,2,1,0,3:T(8,128)}, u32[]{:S(2)}, u32[]{:S(2)}) async-start(f32[2,5,8,32,128]{4,2,1,0,3:T(8,128)} %fusion.7), calls=%async_computation.1 | async-start | bytes 2621440 | tf_op jit(solution)/shard_map/all_to_all | solution.py:95
  36.7 0.7 copy.22
  37.4 18.0 %all-to-all-done.1 = f32[2,5,8,32,128]{4,2,1,0,3:T(8,128)} async-done(((f32[2,5,8,32,128]{4,2,1,0,3:T(8,128)}), f32[2,5,8,32,128]{4,2,1,0,3:T(8,128)}, u32[]{:S(2)}, u32[]{:S(2)}) %all-to-all-start.1) | async-done | bytes 1310752 | tf_op jit(solution)/shard_map/all_to_all | solution.py:95
  55.4 2.0 %copy.33 = f32[2,5,8,4,8,128]{5,0,3,4,2,1:T(2,128)S(1)} copy(f32[2,5,8,4,8,128]{5,2,1,0,4,3:T(8,128)} %bitcast.4) | data formatting | bytes 2621440 | tf_op jit(solution)/shard_map/all_to_all | solution.py:95
  57.4 1.3 fusion.2
  59.5 0.8 fusion.143
  60.7 0.8 fusion.142
  61.4 1.9 %collective-permute-start.5 = (f32[8,5,1,8,128]{4,0,3,2,1:T(8,128)}, f32[8,5,1,8,128]{4,0,3,2,1:T(8,128)}, u32[]{:S(2)}, u32[]{:S(2)}) collective-permute-start(f32[8,5,1,8,128]{4,0,3,2,1:T(8,128)} %get-tuple-element.19), channel_id=1, source_target_pairs={{0,1},{1,2},{2,3},{3,4},{4,5},{5,6},{6,7},{7,8},{8,9},{9,10},{10,1... | collective-permute-start | bytes 491528 | tf_op jit(solution)/shard_map/ppermute | solution.py:22
  63.3 8.9 %collective-permute-start.4 = (f32[8,5,1,8,128]{4,0,3,2,1:T(8,128)}, f32[8,5,1,8,128]{4,0,3,2,1:T(8,128)}, u32[]{:S(2)}, u32[]{:S(2)}) collective-permute-start(f32[8,5,1,8,128]{4,0,3,2,1:T(8,128)} %get-tuple-element.20), channel_id=1, source_target_pairs={{1,0},{2,1},{3,2},{4,3},{5,4},{6,5},{7,6},{8,7},{9,8},{10,9},{11,1... | collective-permute-start | bytes 491528 | tf_op jit(solution)/shard_map/ppermute | solution.py:23
  72.2 2.0 %collective-permute-start.2 = (f32[8,5,8,1,128]{4,0,3,2,1:T(8,128)}, f32[8,5,8,1,128]{4,0,3,2,1:T(8,128)}, u32[]{:S(2)}, u32[]{:S(2)}) collective-permute-start(f32[8,5,8,1,128]{4,0,3,2,1:T(8,128)} %get-tuple-element.17), channel_id=1, source_target_pairs={{0,64},{64,128},{128,192},{1,65},{65,129},{129,193},{2,66},{66,130... | collective-permute-start | bytes 491528 | tf_op jit(solution)/shard_map/ppermute | solution.py:22
  74.2 1.5 collective-permute-start.3
  75.6 0.8 constant_dynamic-slice_fusion
  76.4 0.9 pad.49
  77.4 0.9 pad.48
  78.3 4.4 %select_maximum_fusion.12 = f32[8,5,10,10,130]{4,0,3,2,1:T(8,128)S(1)} fusion(f32[8,5,1,10,128]{4,0,3,2,1:T(8,128)S(1)} %pad.48, f32[8,5,1,10,128]{4,0,3,2,1:T(8,128)S(1)} %pad.49, f32[8,5,8,1,128]{4,0,3,2,1:T(8,128)} %collective-permute-done.3, f32[8,5,8,8,128]{4,0,3,2,1:T(8,128)} %copy-done, f32[8,5,8,1,128]{4,0,3,2,1:T(8,128)} %collective-permute-done.2), kind=kLoop, calls=%fused_computation.18 | loop fusion | flops 6240000 | bytes 4128000 | tf_op jit(solution)/shard_map/concatenate | solution.py:29
  82.8 3.5 %fusion.24 = f32[8,5,8,8,128]{4,0,3,2,1:T(8,128)S(1)} fusion(f32[8,5,10,10,130]{4,0,3,2,1:T(8,128)S(1)} %select_maximum_fusion.12, f32[8,5,8,8,128]{4,0,3,2,1:T(8,128)S(1)} %copy-done.1, f32[8,5,8,1,128]{4,0,3,2,1:T(8,128)} %collective-permute-done.2, f32[8,5,8,1,128]{4,0,3,2,1:T(8,128)} %collective-permute-done.3, f32[8,5,1,10,128]{4,0,3,2,1:T(8,128)S(1)} %pad.49, ...), kind=kOutput, calls=%fused_computation.84 | convolution fusion | flops 36701504 | bytes 8634368 | tf_op jit(solution)/shard_map/dot_general | solution.py:71
  87.3 1.9 %collective-permute-start.9 = (f32[8,5,1,8,128]{4,0,3,2,1:T(8,128)S(1)}, f32[8,5,1,8,128]{4,0,3,2,1:T(8,128)S(1)}, u32[]{:S(2)}, u32[]{:S(2)}) collective-permute-start(f32[8,5,1,8,128]{4,0,3,2,1:T(8,128)S(1)} %get-tuple-element.15), channel_id=1, source_target_pairs={{0,1},{1,2},{2,3},{3,4},{4,5},{5,6},{6,7},{7,8},{8,9},{9,10},{10,1... | collective-permute-start | bytes 491528 | tf_op jit(solution)/shard_map/ppermute | solution.py:22
  89.3 8.1 %collective-permute-start.8 = (f32[8,5,1,8,128]{4,0,3,2,1:T(8,128)S(1)}, f32[8,5,1,8,128]{4,0,3,2,1:T(8,128)S(1)}, u32[]{:S(2)}, u32[]{:S(2)}) collective-permute-start(f32[8,5,1,8,128]{4,0,3,2,1:T(8,128)S(1)} %get-tuple-element.16), channel_id=1, source_target_pairs={{1,0},{2,1},{3,2},{4,3},{5,4},{6,5},{7,6},{8,7},{9,8},{10,9},{11,1... | collective-permute-start | bytes 491528 | tf_op jit(solution)/shard_map/ppermute | solution.py:23
  97.4 5.4 %collective-permute-start.6 = (f32[8,5,8,1,128]{4,0,3,2,1:T(8,128)S(1)}, f32[8,5,8,1,128]{4,0,3,2,1:T(8,128)S(1)}, u32[]{:S(2)}, u32[]{:S(2)}) collective-permute-start(f32[8,5,8,1,128]{4,0,3,2,1:T(8,128)S(1)} %get-tuple-element.13), channel_id=1, source_target_pairs={{0,64},{64,128},{128,192},{1,65},{65,129},{129,193},{2,66},{66,130... | collective-permute-start | bytes 491528 | tf_op jit(solution)/shard_map/ppermute | solution.py:22
  102.8 1.3 collective-permute-start.7
  104.2 1.9 %collective-permute-done.7 = f32[8,5,8,1,128]{4,0,3,2,1:T(8,128)S(1)} collective-permute-done((f32[8,5,8,1,128]{4,0,3,2,1:T(8,128)S(1)}, f32[8,5,8,1,128]{4,0,3,2,1:T(8,128)S(1)}, u32[]{:S(2)}, u32[]{:S(2)}) %collective-permute-start.7) | collective-permute-done | bytes 163872 | tf_op jit(solution)/shard_map/ppermute | solution.py:23
  106.1 2.8 %select_maximum_fusion.8 = f32[8,5,10,10,130]{4,0,3,2,1:T(8,128)S(1)} fusion(f32[8,5,1,10,128]{4,0,3,2,1:T(8,128)S(1)} %pad.51, f32[8,5,1,10,128]{4,0,3,2,1:T(8,128)S(1)} %pad.52, f32[8,5,8,1,128]{4,0,3,2,1:T(8,128)S(1)} %collective-permute-done.7, f32[8,5,8,8,128]{4,0,3,2,1:T(8,128)S(1)} %add_dynamic-update-slice_fusion.15, ...), kind=kLoop, calls=%fused_computation.14 | loop fusion | flops 6240000 | bytes 4128000 | tf_op jit(solution)/shard_map/concatenate | solution.py:29
  108.9 2.0 %fusion.19 = f32[8,5,8,8,128]{4,0,3,2,1:T(8,128)S(1)} fusion(f32[8,5,10,10,130]{4,0,3,2,1:T(8,128)S(1)} %select_maximum_fusion.8, f32[8,5,8,8,128]{4,0,3,2,1:T(8,128)S(1)} %add_dynamic-update-slice_fusion.15, f32[8,5,8,1,128]{4,0,3,2,1:T(8,128)S(1)} %collective-permute-done.6, f32[8,5,8,1,128]{4,0,3,2,1:T(8,128)S(1)} %collective-permute-done.7, ...), kind=kOutput, calls=%fused_computation.69 | convolution fusion | flops 36701504 | bytes 8634368 | tf_op jit(solution)/shard_map/dot_general | solution.py:71
  112.0 1.9 %collective-permute-start.13 = (f32[8,5,1,8,128]{4,0,3,2,1:T(8,128)S(1)}, f32[8,5,1,8,128]{4,0,3,2,1:T(8,128)S(1)}, u32[]{:S(2)}, u32[]{:S(2)}) collective-permute-start(f32[8,5,1,8,128]{4,0,3,2,1:T(8,128)S(1)} %get-tuple-element.11), channel_id=1, source_target_pairs={{0,1},{1,2},{2,3},{3,4},{4,5},{5,6},{6,7},{7,8},{8,9},{9,10},{10,1... | collective-permute-start | bytes 491528 | tf_op jit(solution)/shard_map/ppermute | solution.py:22
  114.0 8.1 %collective-permute-start.12 = (f32[8,5,1,8,128]{4,0,3,2,1:T(8,128)S(1)}, f32[8,5,1,8,128]{4,0,3,2,1:T(8,128)S(1)}, u32[]{:S(2)}, u32[]{:S(2)}) collective-permute-start(f32[8,5,1,8,128]{4,0,3,2,1:T(8,128)S(1)} %get-tuple-element.12), channel_id=1, source_target_pairs={{1,0},{2,1},{3,2},{4,3},{5,4},{6,5},{7,6},{8,7},{9,8},{10,9},{11,1... | collective-permute-start | bytes 491528 | tf_op jit(solution)/shard_map/ppermute | solution.py:23
  122.1 6.7 %collective-permute-start.10 = (f32[8,5,8,1,128]{4,0,3,2,1:T(8,128)S(1)}, f32[8,5,8,1,128]{4,0,3,2,1:T(8,128)S(1)}, u32[]{:S(2)}, u32[]{:S(2)}) collective-permute-start(f32[8,5,8,1,128]{4,0,3,2,1:T(8,128)S(1)} %get-tuple-element.9), channel_id=1, source_target_pairs={{0,64},{64,128},{128,192},{1,65},{65,129},{129,193},{2,66},{66,130... | collective-permute-start | bytes 491528 | tf_op jit(solution)/shard_map/ppermute | solution.py:22
  128.8 1.5 collective-permute-start.11
  130.4 1.7 collective-permute-done.11
  132.1 2.8 %select_maximum_fusion.4 = f32[8,5,10,10,130]{4,0,3,2,1:T(8,128)S(1)} fusion(f32[8,5,1,10,128]{4,0,3,2,1:T(8,128)S(1)} %pad.54, f32[8,5,1,10,128]{4,0,3,2,1:T(8,128)S(1)} %pad.55, f32[8,5,8,1,128]{4,0,3,2,1:T(8,128)S(1)} %collective-permute-done.11, f32[8,5,8,8,128]{4,0,3,2,1:T(8,128)S(1)} %add_dynamic-update-slice_fusion.10, ...), kind=kLoop, calls=%fused_computation.10 | loop fusion | flops 6240000 | bytes 4128000 | tf_op jit(solution)/shard_map/concatenate | solution.py:29
  134.9 2.0 %fusion.14 = f32[8,5,8,8,128]{4,0,3,2,1:T(8,128)S(1)} fusion(f32[8,5,10,10,130]{4,0,3,2,1:T(8,128)S(1)} %select_maximum_fusion.4, f32[8,5,8,8,128]{4,0,3,2,1:T(8,128)S(1)} %add_dynamic-update-slice_fusion.10, f32[8,5,8,1,128]{4,0,3,2,1:T(8,128)S(1)} %collective-permute-done.10, f32[8,5,8,1,128]{4,0,3,2,1:T(8,128)S(1)} %collective-permute-done.11, ...), kind=kOutput, calls=%fused_computation.54 | convolution fusion | flops 36701504 | bytes 8634368 | tf_op jit(solution)/shard_map/dot_general | solution.py:71
  138.0 1.9 %collective-permute-start.17 = (f32[8,5,1,8,128]{4,0,3,2,1:T(8,128)S(1)}, f32[8,5,1,8,128]{4,0,3,2,1:T(8,128)S(1)}, u32[]{:S(2)}, u32[]{:S(2)}) collective-permute-start(f32[8,5,1,8,128]{4,0,3,2,1:T(8,128)S(1)} %get-tuple-element.7), channel_id=1, source_target_pairs={{0,1},{1,2},{2,3},{3,4},{4,5},{5,6},{6,7},{7,8},{8,9},{9,10},{10,1... | collective-permute-start | bytes 491528 | tf_op jit(solution)/shard_map/ppermute | solution.py:22
  140.0 8.1 %collective-permute-start.16 = (f32[8,5,1,8,128]{4,0,3,2,1:T(8,128)S(1)}, f32[8,5,1,8,128]{4,0,3,2,1:T(8,128)S(1)}, u32[]{:S(2)}, u32[]{:S(2)}) collective-permute-start(f32[8,5,1,8,128]{4,0,3,2,1:T(8,128)S(1)} %get-tuple-element.8), channel_id=1, source_target_pairs={{1,0},{2,1},{3,2},{4,3},{5,4},{6,5},{7,6},{8,7},{9,8},{10,9},{11,1... | collective-permute-start | bytes 491528 | tf_op jit(solution)/shard_map/ppermute | solution.py:23
  148.1 6.6 %collective-permute-start.14 = (f32[8,5,8,1,128]{4,0,3,2,1:T(8,128)S(1)}, f32[8,5,8,1,128]{4,0,3,2,1:T(8,128)S(1)}, u32[]{:S(2)}, u32[]{:S(2)}) collective-permute-start(f32[8,5,8,1,128]{4,0,3,2,1:T(8,128)S(1)} %get-tuple-element.5), channel_id=1, source_target_pairs={{0,64},{64,128},{128,192},{1,65},{65,129},{129,193},{2,66},{66,130... | collective-permute-start | bytes 491528 | tf_op jit(solution)/shard_map/ppermute | solution.py:22
  154.7 1.3 collective-permute-start.15
  156.1 1.9 %collective-permute-done.15 = f32[8,5,8,1,128]{4,0,3,2,1:T(8,128)S(1)} collective-permute-done((f32[8,5,8,1,128]{4,0,3,2,1:T(8,128)S(1)}, f32[8,5,8,1,128]{4,0,3,2,1:T(8,128)S(1)}, u32[]{:S(2)}, u32[]{:S(2)}) %collective-permute-start.15) | collective-permute-done | bytes 163872 | tf_op jit(solution)/shard_map/ppermute | solution.py:23
  158.0 2.8 %select_maximum_fusion = f32[8,5,10,10,130]{4,0,3,2,1:T(8,128)S(1)} fusion(f32[8,5,1,10,128]{4,0,3,2,1:T(8,128)S(1)} %pad.57, f32[8,5,1,10,128]{4,0,3,2,1:T(8,128)S(1)} %pad.58, f32[8,5,8,1,128]{4,0,3,2,1:T(8,128)S(1)} %collective-permute-done.15, f32[8,5,8,8,128]{4,0,3,2,1:T(8,128)S(1)} %add_dynamic-update-slice_fusion.5, ...), kind=kLoop, calls=%fused_computation.6 | loop fusion | flops 6240000 | bytes 4128000 | tf_op jit(solution)/shard_map/concatenate | solution.py:29
  160.8 2.0 %fusion.9 = f32[8,5,8,8,128]{4,0,3,2,1:T(8,128)S(1)} fusion(f32[8,5,10,10,130]{4,0,3,2,1:T(8,128)S(1)} %select_maximum_fusion, f32[8,5,8,8,128]{4,0,3,2,1:T(8,128)S(1)} %add_dynamic-update-slice_fusion.5, f32[8,5,8,1,128]{4,0,3,2,1:T(8,128)S(1)} %collective-permute-done.14, f32[8,5,8,1,128]{4,0,3,2,1:T(8,128)S(1)} %collective-permute-done.15, ...), kind=kOutput, calls=%fused_computation.39 | convolution fusion | flops 36701504 | bytes 8634368 | tf_op jit(solution)/shard_map/dot_general | solution.py:71
  164.4 25.1 %all_to_all.54 = f32[8,5,8,8,128]{4,3,2,1,0:T(8,128)S(1)} all-to-all(f32[8,5,8,8,128]{4,3,2,1,0:T(8,128)S(1)} %copy.34), channel_id=1, replica_groups=mesh['inst'=4,'cells'=64] {'inst'}, dimensions={0} | all-to-all | bytes 2621440 | tf_op jit(solution)/shard_map/all_to_all | solution.py:102
  189.4 1.2 copy.39
  (68 shorter events, 6.4 us)
Async XLA Ops:
  3.1 17.4 %copy-start.4 = (f32[8,32,128]{2,1,0:T(8,128)S(1)}, f32[8,32,128]{2,1,0:T(8,128)}, u32[]{:S(2)}) copy-start(f32[8,32,128]{2,1,0:T(8,128)} %param.6) | copy-start | bytes 393220
  3.1 29.0 %all-to-all-start = ((f32[2,5,8,32,128]{4,2,1,0,3:T(8,128)}), f32[2,5,8,32,128]{4,2,1,0,3:T(8,128)S(1)}, u32[]{:S(2)}, u32[]{:S(2)}) async-start(f32[2,5,8,32,128]{4,2,1,0,3:T(8,128)} %copy.21), calls=%async_computation | async-start | bytes 2621440 | tf_op jit(solution)/shard_map/all_to_all | solution.py:94
  7.9 15.7 %collective-permute-start.1 = (f32[2,5,1,32,128]{4,3,2,1,0:T(8,128)S(1)}, f32[2,5,1,32,128]{4,3,2,1,0:T(8,128)S(1)}, u32[]{:S(2)}, u32[]{:S(2)}) collective-permute-start(f32[2,5,1,32,128]{4,3,2,1,0:T(8,128)S(1)} %get-tuple-element.21), channel_id=1, source_target_pairs={{0,1},{1,2},{2,3},{3,4},{4,5},{5,6},{6,7},{7,8},{8,9},{9,10},{10,1... | collective-permute-start | bytes 491528 | tf_op jit(solution)/shard_map/ppermute | solution.py:41
  11.7 13.0 %collective-permute-start = (f32[2,5,1,32,128]{4,3,2,1,0:T(8,128)S(1)}, f32[2,5,1,32,128]{4,3,2,1,0:T(8,128)S(1)}, u32[]{:S(2)}, u32[]{:S(2)}) collective-permute-start(f32[2,5,1,32,128]{4,3,2,1,0:T(8,128)S(1)} %get-tuple-element.22), channel_id=1, source_target_pairs={{1,0},{2,1},{3,2},{4,3},{5,4},{6,5},{7,6},{8,7},{9,8},{10,9},{11,1... | collective-permute-start | bytes 491528 | tf_op jit(solution)/shard_map/ppermute | solution.py:42
  24.8 1.9 %copy-start.2 = (f32[2,5,8,32,128]{4,3,2,1,0:T(8,128)S(1)}, f32[2,5,8,32,128]{4,3,2,1,0:T(8,128)}, u32[]{:S(2)}) copy-start(f32[2,5,8,32,128]{4,3,2,1,0:T(8,128)} %param.5) | copy-start | bytes 3932164
  32.2 4.4 %copy-start.3 = (f32[5,5,8,8,128]{4,3,2,1,0:T(8,128)S(1)}, f32[5,5,8,8,128]{4,3,2,1,0:T(8,128)}, u32[]{:S(2)}) copy-start(f32[5,5,8,8,128]{4,3,2,1,0:T(8,128)} %param.7) | copy-start | bytes 2457604
  32.2 23.2 %all-to-all-start.1 = ((f32[2,5,8,32,128]{4,2,1,0,3:T(8,128)}), f32[2,5,8,32,128]{4,2,1,0,3:T(8,128)}, u32[]{:S(2)}, u32[]{:S(2)}) async-start(f32[2,5,8,32,128]{4,2,1,0,3:T(8,128)} %fusion.7), calls=%async_computation.1 | async-start | bytes 2621440 | tf_op jit(solution)/shard_map/all_to_all | solution.py:95
  59.5 1.2 copy-start
  61.4 15.0 %collective-permute-start.5 = (f32[8,5,1,8,128]{4,0,3,2,1:T(8,128)}, f32[8,5,1,8,128]{4,0,3,2,1:T(8,128)}, u32[]{:S(2)}, u32[]{:S(2)}) collective-permute-start(f32[8,5,1,8,128]{4,0,3,2,1:T(8,128)} %get-tuple-element.19), channel_id=1, source_target_pairs={{0,1},{1,2},{2,3},{3,4},{4,5},{5,6},{6,7},{7,8},{8,9},{9,10},{10,1... | collective-permute-start | bytes 491528 | tf_op jit(solution)/shard_map/ppermute | solution.py:22
  63.3 14.0 %collective-permute-start.4 = (f32[8,5,1,8,128]{4,0,3,2,1:T(8,128)}, f32[8,5,1,8,128]{4,0,3,2,1:T(8,128)}, u32[]{:S(2)}, u32[]{:S(2)}) collective-permute-start(f32[8,5,1,8,128]{4,0,3,2,1:T(8,128)} %get-tuple-element.20), channel_id=1, source_target_pairs={{1,0},{2,1},{3,2},{4,3},{5,4},{6,5},{7,6},{8,7},{9,8},{10,9},{11,1... | collective-permute-start | bytes 491528 | tf_op jit(solution)/shard_map/ppermute | solution.py:23
  72.2 6.1 %collective-permute-start.2 = (f32[8,5,8,1,128]{4,0,3,2,1:T(8,128)}, f32[8,5,8,1,128]{4,0,3,2,1:T(8,128)}, u32[]{:S(2)}, u32[]{:S(2)}) collective-permute-start(f32[8,5,8,1,128]{4,0,3,2,1:T(8,128)} %get-tuple-element.17), channel_id=1, source_target_pairs={{0,64},{64,128},{128,192},{1,65},{65,129},{129,193},{2,66},{66,130... | collective-permute-start | bytes 491528 | tf_op jit(solution)/shard_map/ppermute | solution.py:22
  74.2 4.2 %collective-permute-start.3 = (f32[8,5,8,1,128]{4,0,3,2,1:T(8,128)}, f32[8,5,8,1,128]{4,0,3,2,1:T(8,128)}, u32[]{:S(2)}, u32[]{:S(2)}) collective-permute-start(f32[8,5,8,1,128]{4,0,3,2,1:T(8,128)} %get-tuple-element.18), channel_id=1, source_target_pairs={{64,0},{128,64},{192,128},{65,1},{129,65},{193,129},{66,2},{130,66... | collective-permute-start | bytes 491528 | tf_op jit(solution)/shard_map/ppermute | solution.py:23
  78.3 4.5 %copy-start.1 = (f32[8,5,8,8,128]{4,0,3,2,1:T(8,128)S(1)}, f32[8,5,8,8,128]{4,0,3,2,1:T(8,128)}, u32[]{:S(2)}) copy-start(f32[8,5,8,8,128]{4,0,3,2,1:T(8,128)} %copy-done) | copy-start | bytes 3932164
  87.3 16.8 %collective-permute-start.9 = (f32[8,5,1,8,128]{4,0,3,2,1:T(8,128)S(1)}, f32[8,5,1,8,128]{4,0,3,2,1:T(8,128)S(1)}, u32[]{:S(2)}, u32[]{:S(2)}) collective-permute-start(f32[8,5,1,8,128]{4,0,3,2,1:T(8,128)S(1)} %get-tuple-element.15), channel_id=1, source_target_pairs={{0,1},{1,2},{2,3},{3,4},{4,5},{5,6},{6,7},{7,8},{8,9},{9,10},{10,1... | collective-permute-start | bytes 491528 | tf_op jit(solution)/shard_map/ppermute | solution.py:22
  89.3 14.9 %collective-permute-start.8 = (f32[8,5,1,8,128]{4,0,3,2,1:T(8,128)S(1)}, f32[8,5,1,8,128]{4,0,3,2,1:T(8,128)S(1)}, u32[]{:S(2)}, u32[]{:S(2)}) collective-permute-start(f32[8,5,1,8,128]{4,0,3,2,1:T(8,128)S(1)} %get-tuple-element.16), channel_id=1, source_target_pairs={{1,0},{2,1},{3,2},{4,3},{5,4},{6,5},{7,6},{8,7},{9,8},{10,9},{11,1... | collective-permute-start | bytes 491528 | tf_op jit(solution)/shard_map/ppermute | solution.py:23
  97.4 6.8 %collective-permute-start.6 = (f32[8,5,8,1,128]{4,0,3,2,1:T(8,128)S(1)}, f32[8,5,8,1,128]{4,0,3,2,1:T(8,128)S(1)}, u32[]{:S(2)}, u32[]{:S(2)}) collective-permute-start(f32[8,5,8,1,128]{4,0,3,2,1:T(8,128)S(1)} %get-tuple-element.13), channel_id=1, source_target_pairs={{0,64},{64,128},{128,192},{1,65},{65,129},{129,193},{2,66},{66,130... | collective-permute-start | bytes 491528 | tf_op jit(solution)/shard_map/ppermute | solution.py:22
  102.8 3.3 %collective-permute-start.7 = (f32[8,5,8,1,128]{4,0,3,2,1:T(8,128)S(1)}, f32[8,5,8,1,128]{4,0,3,2,1:T(8,128)S(1)}, u32[]{:S(2)}, u32[]{:S(2)}) collective-permute-start(f32[8,5,8,1,128]{4,0,3,2,1:T(8,128)S(1)} %get-tuple-element.14), channel_id=1, source_target_pairs={{64,0},{128,64},{192,128},{65,1},{129,65},{193,129},{66,2},{130,66... | collective-permute-start | bytes 491528 | tf_op jit(solution)/shard_map/ppermute | solution.py:23
  112.0 18.3 %collective-permute-start.13 = (f32[8,5,1,8,128]{4,0,3,2,1:T(8,128)S(1)}, f32[8,5,1,8,128]{4,0,3,2,1:T(8,128)S(1)}, u32[]{:S(2)}, u32[]{:S(2)}) collective-permute-start(f32[8,5,1,8,128]{4,0,3,2,1:T(8,128)S(1)} %get-tuple-element.11), channel_id=1, source_target_pairs={{0,1},{1,2},{2,3},{3,4},{4,5},{5,6},{6,7},{7,8},{8,9},{9,10},{10,1... | collective-permute-start | bytes 491528 | tf_op jit(solution)/shard_map/ppermute | solution.py:22
  114.0 16.4 %collective-permute-start.12 = (f32[8,5,1,8,128]{4,0,3,2,1:T(8,128)S(1)}, f32[8,5,1,8,128]{4,0,3,2,1:T(8,128)S(1)}, u32[]{:S(2)}, u32[]{:S(2)}) collective-permute-start(f32[8,5,1,8,128]{4,0,3,2,1:T(8,128)S(1)} %get-tuple-element.12), channel_id=1, source_target_pairs={{1,0},{2,1},{3,2},{4,3},{5,4},{6,5},{7,6},{8,7},{9,8},{10,9},{11,1... | collective-permute-start | bytes 491528 | tf_op jit(solution)/shard_map/ppermute | solution.py:23
  122.1 8.3 %collective-permute-start.10 = (f32[8,5,8,1,128]{4,0,3,2,1:T(8,128)S(1)}, f32[8,5,8,1,128]{4,0,3,2,1:T(8,128)S(1)}, u32[]{:S(2)}, u32[]{:S(2)}) collective-permute-start(f32[8,5,8,1,128]{4,0,3,2,1:T(8,128)S(1)} %get-tuple-element.9), channel_id=1, source_target_pairs={{0,64},{64,128},{128,192},{1,65},{65,129},{129,193},{2,66},{66,130... | collective-permute-start | bytes 491528 | tf_op jit(solution)/shard_map/ppermute | solution.py:22
  128.8 3.3 %collective-permute-start.11 = (f32[8,5,8,1,128]{4,0,3,2,1:T(8,128)S(1)}, f32[8,5,8,1,128]{4,0,3,2,1:T(8,128)S(1)}, u32[]{:S(2)}, u32[]{:S(2)}) collective-permute-start(f32[8,5,8,1,128]{4,0,3,2,1:T(8,128)S(1)} %get-tuple-element.10), channel_id=1, source_target_pairs={{64,0},{128,64},{192,128},{65,1},{129,65},{193,129},{66,2},{130,66... | collective-permute-start | bytes 491528 | tf_op jit(solution)/shard_map/ppermute | solution.py:23
  138.0 18.0 %collective-permute-start.17 = (f32[8,5,1,8,128]{4,0,3,2,1:T(8,128)S(1)}, f32[8,5,1,8,128]{4,0,3,2,1:T(8,128)S(1)}, u32[]{:S(2)}, u32[]{:S(2)}) collective-permute-start(f32[8,5,1,8,128]{4,0,3,2,1:T(8,128)S(1)} %get-tuple-element.7), channel_id=1, source_target_pairs={{0,1},{1,2},{2,3},{3,4},{4,5},{5,6},{6,7},{7,8},{8,9},{9,10},{10,1... | collective-permute-start | bytes 491528 | tf_op jit(solution)/shard_map/ppermute | solution.py:22
  140.0 16.1 %collective-permute-start.16 = (f32[8,5,1,8,128]{4,0,3,2,1:T(8,128)S(1)}, f32[8,5,1,8,128]{4,0,3,2,1:T(8,128)S(1)}, u32[]{:S(2)}, u32[]{:S(2)}) collective-permute-start(f32[8,5,1,8,128]{4,0,3,2,1:T(8,128)S(1)} %get-tuple-element.8), channel_id=1, source_target_pairs={{1,0},{2,1},{3,2},{4,3},{5,4},{6,5},{7,6},{8,7},{9,8},{10,9},{11,1... | collective-permute-start | bytes 491528 | tf_op jit(solution)/shard_map/ppermute | solution.py:23
  148.1 8.0 %collective-permute-start.14 = (f32[8,5,8,1,128]{4,0,3,2,1:T(8,128)S(1)}, f32[8,5,8,1,128]{4,0,3,2,1:T(8,128)S(1)}, u32[]{:S(2)}, u32[]{:S(2)}) collective-permute-start(f32[8,5,8,1,128]{4,0,3,2,1:T(8,128)S(1)} %get-tuple-element.5), channel_id=1, source_target_pairs={{0,64},{64,128},{128,192},{1,65},{65,129},{129,193},{2,66},{66,130... | collective-permute-start | bytes 491528 | tf_op jit(solution)/shard_map/ppermute | solution.py:22
  154.7 3.3 %collective-permute-start.15 = (f32[8,5,8,1,128]{4,0,3,2,1:T(8,128)S(1)}, f32[8,5,8,1,128]{4,0,3,2,1:T(8,128)S(1)}, u32[]{:S(2)}, u32[]{:S(2)}) collective-permute-start(f32[8,5,8,1,128]{4,0,3,2,1:T(8,128)S(1)} %get-tuple-element.6), channel_id=1, source_target_pairs={{64,0},{128,64},{192,128},{65,1},{129,65},{193,129},{66,2},{130,66... | collective-permute-start | bytes 491528 | tf_op jit(solution)/shard_map/ppermute | solution.py:23
where the time goes:
time: 192 us; the launch traced here: 191 us
  starting transfers between devices  88 us (46%)
  waiting for transfers between devices  27.4 us (14%)
  other arithmetic  25.2 us (13%)
  blocking collectives  25.1 us (13%)
  local copies, waits for them, and re-layouts  13.6 us (7%)
  matrix products  10.8 us (6%)
    ppermute x8, starting transfers between devices, extended(): lax.ppermute(initial, axis, [(b, a) for a, b in up])  38.8 us
    ppermute x8, starting transfers between devices, extended(): lax.ppermute(last, axis, up)  28.3 us
    all_to_all x1, blocking collectives, on_device(): lax.all_to_all(moved_state + update, 'inst', split_axis=0, concat_axis=3,...  25.1 us
    all_to_all x1, waiting for transfers between devices, on_device(): lax.all_to_all(local_part, 'inst', split_axis=3, concat_axis=0, tiled=True)  18 us
    concatenate x4, other arithmetic, extended(): jnp.concatenate([jnp.pad(low, around), shard, jnp.pad(high, around)], axi...  12.9 us
    dot_general x5, matrix products, spectral_term(): product = jnp.dot(matrix, flat, precision=lax.Precision.HIGHEST)  10.8 us
    ppermute x1, starting transfers between devices, extended_2(): after = lax.ppermute(initial, axis, down)  8.84 us
    ppermute x8, waiting for transfers between devices, extended(): lax.ppermute(initial, axis, [(b, a) for a, b in up])  5.52 us
  transfers between devices with their start and end apart: 20, of which 6 were waited for; matrix products, arithmetic and copies ran while one was open for 6% of the time, Pallas kernels for 0%

commit v1 on v0

v1 whole, which is shorter than its diff:
```python
import math

import jax
import jax.numpy as jnp
from jax import lax
from jax.experimental import pallas as pl
from jax.experimental.pallas import tpu as pltpu
from jax.sharding import PartitionSpec as P

AXES = ("inst", "cells")
NV = 5
RW = 20
BW = 24
F32 = jnp.float32


def place():
    index = lax.axis_index("inst")
    return index % 2, index // 2


def m8(value):
    return pl.multiple_of(value, 8)


def plane_of(s, core):
    return s + core * (7 - 2 * s)


def low_half():
    return lax.broadcasted_iota(jnp.int32, (8, 128), 0) < 4


def pack_rows(src, dst, offset, k, planes, core, chip):
    to_core = core ^ (k & 1)
    to_chip = chip ^ (k >> 1)
    low = low_half()

    def step(ev, carry):
        halo = []
        for si, s in enumerate(planes):
            base = (ev * 8 + plane_of(s, to_core)) * 32
            for t in range(2):
                dst[pl.ds(m8(offset + (ev * 2 + si) * 16 + 8 * t), 8), :] = src[
                    pl.ds(m8(base + 16 * to_chip + 8 * t), 8), :
                ]
            halo.append(src[pl.ds(m8(base + 16 - 8 * to_chip), 8), :])
        first, second = halo
        upper = jnp.where(low, first, pltpu.roll(second, 4, 0))
        lower = jnp.where(low, pltpu.roll(first, 4, 0), second)
        dst[pl.ds(m8(offset + 320 + ev * 8), 8), :] = jnp.where(to_chip == 1, lower, upper)
        return carry

    lax.fori_loop(0, 10, step, 0)


def state_kernel(f, o0, o1, o2, o3, first, last):
    core, chip = place()
    for k, out in ((2, o2), (3, o3), (1, o1), (0, o0)):
        pack_rows(f, out, 0, k, (0, 1), core, chip)
        pack_rows(f, out, 400, k, (2, 3), core, chip)

    def step(ev, carry):
        for t in range(4):
            first[pl.ds(m8(ev * 32 + 8 * t), 8), :] = f[pl.ds(m8(ev * 256 + 8 * t), 8), :]
            last[pl.ds(m8(ev * 32 + 8 * t), 8), :] = f[pl.ds(m8(ev * 256 + 224 + 8 * t), 8), :]
        return carry

    lax.fori_loop(0, 10, step, 0)


def part_kernel(f, g, d, lo, hi, e0, e1, e2, e3, i0, i1, i2, i3, part):
    core, chip = place()
    row = lax.broadcasted_iota(jnp.int32, (32, 128), 0)
    lane = lax.broadcasted_iota(jnp.int32, (32, 128), 1)

    def step(ev, carry):
        for x in range(8):
            own = f[pl.ds(m8((ev * 8 + x) * 32), 32), :]
            before = lo[pl.ds(m8(ev * 32), 32), :] if x == 0 else f[pl.ds(m8((ev * 8 + x - 1) * 32), 32), :]
            after = hi[pl.ds(m8(ev * 32), 32), :] if x == 7 else f[pl.ds(m8((ev * 8 + x + 1) * 32), 32), :]
            beside = before + after
            beside = beside + jnp.where(row == 0, 0.0, pltpu.roll(own, 1, 0))
            beside = beside + jnp.where(row == 31, 0.0, pltpu.roll(own, 31, 0))
            beside = beside + jnp.where(lane == 0, 0.0, pltpu.roll(own, 1, 1))
            beside = beside + jnp.where(lane == 127, 0.0, pltpu.roll(own, 127, 1))
            part[pl.ds(m8((ev * 8 + x) * 32), 32), :] = (
                d[pl.ds(x * 32, 32), :] * (6.0 * own - beside) - g[pl.ds(m8((ev * 8 + x) * 32), 32), :]
            )
        return carry

    lax.fori_loop(0, 10, step, 0)
    for k, out in ((2, e2), (3, e3), (1, e1), (0, e0)):
        pack_rows(part, out, 0, k, (0, 1), core, chip)
    for k, out in ((2, i2), (3, i3), (1, i1), (0, i0)):
        pack_rows(part, out, 0, k, (2, 3), core, chip)


ROOT8 = 1.0 / math.sqrt(8.0)
ROOT2 = 1.0 / math.sqrt(2.0)


def to_modes(pieces, core, chip):
    swapped = core == 1
    sums = [[pieces[a][e] + pieces[a + 2][e] for e in range(2)] for a in range(2)]
    diffs = [[pieces[a][e] - pieces[a + 2][e] for e in range(2)] for a in range(2)]
    s = [jnp.where(swapped, sums[1 - a][e], sums[a][e]) for a in range(2) for e in range(2)]
    d = [jnp.where(swapped, diffs[1 - a][e], diffs[a][e]) for a in range(2) for e in range(2)]
    half = jnp.where(chip == 1, -0.5, 0.5).astype(F32)
    even, odd = s[0] + s[2], s[1] + s[3]
    near, far = (d[1] - d[3]) * ROOT2, (d[1] + d[3]) * ROOT2
    return [
        half * (d[0] + near),
        0.5 * (s[0] - s[2]),
        half * (d[0] - near),
        ROOT8 * (even + odd),
        half * (far + d[2]),
        0.5 * (s[1] - s[3]),
        half * (far - d[2]),
        ROOT8 * (even - odd),
    ]


def from_modes(m):
    c1, c2, c3, m0, s1, s2, s3, m4 = m
    even, odd = ROOT8 * (m0 + m4), ROOT8 * (m0 - m4)
    s = [even + 0.5 * c2, odd + 0.5 * s2, even - 0.5 * c2, odd - 0.5 * s2]
    near, far = (0.5 * ROOT2) * (c1 - c3), (0.5 * ROOT2) * (s1 + s3)
    d = [0.5 * (c1 + c3), near + far, 0.5 * (s1 - s3), far - near]
    return [s[j] + d[j] for j in range(4)] + [s[j] - d[j] for j in range(4)]


def modes_kernel(offset, f0, f1, f2, f3, p0, p1, p2, p3, out):
    core, chip = place()
    fs, ps = (f0, f1, f2, f3), (p0, p1, p2, p3)

    def residual(row):
        mf = to_modes([[f[pl.ds(m8(offset + row + e * shift), 8), :] for e in range(2)] for f in fs], core, chip)
        mp = to_modes([[p[pl.ds(m8(row + e * shift), 8), :] for e in range(2)] for p in ps], core, chip)
        for k in range(3):
            mp[k] = mp[k] + (k + 1.0) * mf[4 + k]
            mp[4 + k] = mp[4 + k] - (k + 1.0) * mf[k]
        return mp

    def step(v, carry):
        nonlocal shift
        for si in range(2):
            for t in range(2):
                shift = 160
                modes = residual((v * 2 + si) * 16 + 8 * t)
                start = (si * RW + 4 * chip + 8 * t) * 40 + v * 8
                for m in range(8):
                    out[pl.ds(start + m, 8, stride=40), :] = modes[m]
        shift = 40
        modes = residual(320 + v * 8)
        for si in range(2):
            start = (si * RW + 16 * (1 - chip)) * 40 + v * 8
            for m in range(8):
                out[pl.ds(start + m, 4, stride=40), :] = modes[m][4 * si : 4 * si + 4, :]
        return carry

    shift = 160
    lax.fori_loop(0, NV, step, 0)


def inverse_pack_kernel(b, own, other, halo2, halo3):
    core, chip = place()
    low = low_half()

    def step(j, carry):
        for k, full, halo in ((0, own, halo2), (1, other, halo3)):
            rows = [b[pl.ds(m8((j * 8 + plane_of(s, core ^ k)) * 8), 8), :] for s in range(4)]
            for s in range(4):
                full[pl.ds(m8((j * 4 + s) * 8), 8), :] = rows[s]
            for a in range(2):
                first, second = rows[2 * a], rows[2 * a + 1]
                upper = jnp.where(low, first, pltpu.roll(second, 4, 0))
                lower = jnp.where(low, pltpu.roll(first, 4, 0), second)
                halo[pl.ds(m8((j * 2 + a) * 8), 8), :] = jnp.where(chip == 0, lower, upper)
        return carry

    lax.fori_loop(0, 25, step, 0)


def inverse_window_kernel(own, other, halo2, halo3, d, edge, inner):
    core, chip = place()
    low = low_half()
    straight = core == chip

    def step(j, carry):
        for s in range(4):
            out, base = (edge, inner)[s // 2], (j * 2 + s % 2) * BW
            out[pl.ds(m8(base + 8 * chip + 8 * core), 8), :] = own[pl.ds(m8((j * 4 + s) * 8), 8), :]
            out[pl.ds(m8(base + 8 * chip + 8 * (1 - core)), 8), :] = other[pl.ds(m8((j * 4 + s) * 8), 8), :]
        for a in range(2):
            at = pl.ds(m8((j * 2 + a) * 8), 8)
            both = jnp.where(straight, halo2[at, :], halo3[at, :])
            turned = pltpu.roll(both, 4, 0)
            out = (edge, inner)[a]
            for si in range(2):
                rows = jnp.where((chip == 0) == (si == 0), both, turned)
                rows = jnp.where(low == (chip == 0), rows, 0.0)
                out[pl.ds(m8((j * 2 + si) * BW + 16 * (1 - chip)), 8), :] = rows
        return carry

    lax.fori_loop(0, 25, step, 0)
    for s in range(4):
        out, base = (edge, inner)[s // 2], (25 * 2 + s % 2) * BW
        out[pl.ds(base, BW), :] = d[pl.ds(m8(plane_of(s, core) * 32 + 8 * chip), BW), :]


class Window:
    def __init__(self, beyond, edge, inner, across):
        self.at = [(beyond, 1), (beyond, 0), (edge, 0), (edge, 1), (inner, 0), (inner, 1), (across, 1), (across, 0)]


def wave_numbers():
    sub = lax.broadcasted_iota(jnp.int32, (8, 128), 0)
    rate = jnp.where(sub < 3, sub + 1, jnp.where(sub < 4, 0, jnp.where(sub < 7, 3 - sub, 0)))
    return rate.astype(F32)


def blocks(ref, s, row, source):
    def entry(j):
        return ref[pl.ds((j * 2 + s) * BW + row, 8, stride=0), :]

    outs = []
    for v in range(NV):
        total = entry(v * NV) * source[0]
        for u in range(1, NV):
            total = total + entry(v * NV + u) * source[u]
        outs.append(total)
    return outs


def sweep(planes, first, count, chip, resid, inv, u_in, write):
    lane = lax.broadcasted_iota(jnp.int32, (8, 128), 1)
    inside_low, inside_high = lane > 0, lane < 127
    rate = wave_numbers()

    def at(x, row, v):
        return u_in[(x * (RW + 2) + row + 1) * NV + v]

    def step(n, carry):
        row = first + n
        before = [at(planes[0] - 1, row, v) for v in range(NV)]
        own = [at(planes[0], row, v) for v in range(NV)]
        for x in planes:
            r_ref, s = resid.at[x]
            b_ref, _ = inv.at[x]
            weight = b_ref[pl.ds((25 * 2 + s) * BW + row + 4 * chip, 8, stride=0), :]
            after = [at(x + 1, row, v) for v in range(NV)]
            source = []
            for v in range(NV):
                w = own[v]
                beside = (before[v] + after[v]) + (at(x, row - 1, v) + at(x, row + 1, v))
                beside = beside + jnp.where(inside_low, pltpu.roll(w, 1, 1), 0.0)
                beside = beside + jnp.where(inside_high, pltpu.roll(w, 127, 1), 0.0)
                turned = r_ref[(s * RW + row) * NV + v] - rate * pltpu.roll(w, 4, 0)
                source.append(turned + weight * beside)
            write(x, row, blocks(b_ref, s, row + 4 * chip, source))
            before, own = own, after
        return carry

    lax.fori_loop(0, count, step, 0)


def clear_rows(u):
    zero = jnp.zeros((8, 128), F32)
    for x in range(8):
        for v in range(NV):
            u[x * (RW + 2) * NV + v] = zero
            u[(x * (RW + 2) + RW + 1) * NV + v] = zero


def into(u):
    def write(x, row, values):
        for v in range(NV):
            u[(x * (RW + 2) + row + 1) * NV + v] = values[v]

    return write


def first_kernel(rx, re, ri, rd, bx, be, bi, bd, edge, inner, u0, u1):
    _, chip = place()
    resid, inv = Window(rx, re, ri, rd), Window(bx, be, bi, bd)
    clear_rows(u0)
    clear_rows(u1)

    def step(row, carry):
        for x in range(8):
            r_ref, s = resid.at[x]
            b_ref, _ = inv.at[x]
            source = [r_ref[(s * RW + row) * NV + v] for v in range(NV)]
            into(u0)(x, row, blocks(b_ref, s, row + 4 * chip, source))
        return carry

    lax.fori_loop(0, RW, step, 0)
    sweep(range(1, 7), chip, RW - 1, chip, resid, inv, u0, into(u1))

    def write(x, row, values):
        out, s = (edge, x - 2) if x < 4 else (inner, x - 4)
        for v in range(NV):
            out[(s * (RW - 2) + row - 2 * chip) * NV + v] = values[v]

    sweep(range(2, 6), 2 * chip, RW - 2, chip, resid, inv, u1, write)


def second_kernel(rx, re, ri, rd, bx, be, bi, bd, ux, ue, ui, ud, o0, o1, o2, o3, u0, u1, last):
    core, chip = place()
    resid, inv = Window(rx, re, ri, rd), Window(bx, be, bi, bd)
    given = Window(ux, ue, ui, ud)
    clear_rows(u0)
    clear_rows(u1)

    def fill(n, carry):
        for x in range(8):
            ref, s = given.at[x]
            for v in range(NV):
                u0[(x * (RW + 2) + n + 2 * chip + 1) * NV + v] = ref[(s * (RW - 2) + n) * NV + v]
        return carry

    lax.fori_loop(0, RW - 2, fill, 0)
    sweep(range(1, 7), 3 * chip, RW - 3, chip, resid, inv, u0, into(u1))

    def write(x, row, values):
        for v in range(NV):
            last[pl.ds(m8((((x - 2) * 16 + row - 4 * chip) * NV + v) * 8), 8), :] = values[v]

    sweep(range(2, 6), 4 * chip, RW - 4, chip, resid, inv, u1, write)

    def unpack(v, carry):
        for s in range(4):
            for t in range(2):
                start = (s * 16 + 8 * t) * 40 + v * 8
                values = from_modes([last[pl.ds(start + m, 8, stride=40), :] for m in range(8)])
                pairs = [values[2 * q : 2 * q + 2] for q in range(4)]
                turned = [[jnp.where(core == 1, pairs[q ^ 1][e], pairs[q][e]) for e in range(2)] for q in range(4)]
                for k, out in enumerate((o0, o1, o2, o3)):
                    for e in range(2):
                        out[pl.ds(m8(((e * NV + v) * 4 + s) * 16 + 8 * t), 8), :] = jnp.where(
                            chip == 1, turned[k ^ 2][e], turned[k][e]
                        )
        return carry

    lax.fori_loop(0, NV, unpack, 0)


def final_kernel(f, w0, w1, w2, w3, out):
    core, chip = place()

    def step(ev, carry):
        for k, w in enumerate((w0, w1, w2, w3)):
            for s in range(4):
                base = (ev * 8 + plane_of(s, core ^ (k & 1))) * 32 + 16 * (chip ^ (k >> 1))
                for t in range(2):
                    at = pl.ds(m8(base + 8 * t), 8)
                    out[at, :] = f[at, :] - w[pl.ds(m8((ev * 4 + s) * 16 + 8 * t), 8), :]
        return carry

    lax.fori_loop(0, 10, step, 0)


def call(kernel, name, shapes, *args, scratch=()):
    return pl.pallas_call(
        kernel,
        name=name,
        out_shape=tuple(jax.ShapeDtypeStruct(s, F32) for s in shapes),
        scratch_shapes=[pltpu.VMEM(s, F32) for s in scratch],
        compiler_params=pltpu.CompilerParams(vmem_limit_bytes=40 * 1024 * 1024),
    )(*args)


def exchanges(cells):
    def pairs(move):
        found = []
        for i in range(4):
            for c in range(cells):
                target = move(i, c)
                if target is not None and 0 <= target[1] < cells:
                    found.append((i * cells + c, target[0] * cells + target[1]))
        return found

    return {
        "core": pairs(lambda i, c: (i ^ 1, c)),
        "chip": pairs(lambda i, c: (i ^ 2, c)),
        "both": pairs(lambda i, c: (i ^ 3, c)),
        "up": pairs(lambda i, c: (i, c + 1)),
        "down": pairs(lambda i, c: (i, c - 1)),
        "next": pairs(lambda i, c: (i ^ 1, c - 1 if i % 2 == 0 else c + 1)),
        "halo2": pairs(lambda i, c: (i ^ 2, c) if i in (1, 2) else None),
        "halo3": pairs(lambda i, c: (i ^ 3, c) if i in (1, 2) else None),
    }


def on_device(flow_state, forcing, diffusion, block_inverse):
    routes = exchanges(lax.axis_size("cells"))

    def send(value, route):
        return lax.ppermute(value, AXES, routes[route])

    f = flow_state.reshape(2560, 128)
    g = forcing.reshape(2560, 128)
    d = diffusion.reshape(256, 128)
    b = block_inverse.reshape(1600, 128)

    f0, f1, f2, f3, low, high = call(state_kernel, "state", [(800, 128)] * 4 + [(320, 128)] * 2, f)
    lo, hi = send(high, "up"), send(low, "down")
    f2, f3, f1 = send(f2, "chip"), send(f3, "both"), send(f1, "core")

    own, other, halo2, halo3 = call(
        inverse_pack_kernel, "inverse_pack", [(800, 128)] * 2 + [(400, 128)] * 2, b
    )
    other, halo2, halo3 = send(other, "core"), send(halo2, "halo2"), send(halo3, "halo3")

    parts = call(part_kernel, "part", [(400, 128)] * 8, f, g, d, lo, hi, scratch=[(2560, 128)])
    e0, e1, e2, e3, i0, i1, i2, i3 = parts
    e2, e3, e1 = send(e2, "chip"), send(e3, "both"), send(e1, "core")
    i2, i3, i1 = send(i2, "chip"), send(i3, "both"), send(i1, "core")

    be, bi = call(inverse_window_kernel, "inverse_window", [(26 * 2 * BW, 128)] * 2, own, other, halo2, halo3, d)
    bx, bd = send(be, "next"), send(bi, "core")

    (re,) = call(lambda *refs: modes_kernel(0, *refs), "modes_edge", [(2 * RW * 40, 128)], f0, f1, f2, f3, e0, e1, e2, e3)
    rx = send(re, "next")
    (ri,) = call(lambda *refs: modes_kernel(400, *refs), "modes_inner", [(2 * RW * 40, 128)], f0, f1, f2, f3, i0, i1, i2, i3)
    rd = send(ri, "core")

    resid = [r.reshape(2 * RW * NV, 8, 128) for r in (rx, re, ri, rd)]
    inv = (bx, be, bi, bd)
    u_shape = (8 * (RW + 2) * NV, 8, 128)
    ue, ui = call(
        first_kernel, "first", [(2 * (RW - 2) * NV, 8, 128)] * 2, *resid, *inv, scratch=[u_shape] * 2
    )
    ux, ud = send(ue, "next"), send(ui, "core")
    w0, w1, w2, w3 = call(
        second_kernel,
        "second",
        [(640, 128)] * 4,
        *resid,
        *inv,
        ux,
        ue,
        ui,
        ud,
        scratch=[u_shape] * 2 + [(4 * 16 * 40, 128)],
    )
    w2, w3, w1 = send(w2, "chip"), send(w3, "both"), send(w1, "core")
    (out,) = call(final_kernel, "final", [(2560, 128)], f, w0, w1, w2, w3)
    return out.reshape(flow_state.shape)


def solution(mesh):
    in_specs = (
        P("inst", None, "cells", None, None),
        P("inst", None, "cells", None, None),
        P("cells", None, None),
        P(None, None, "cells", "inst", None),
    )
    out_specs = P("inst", None, "cells", None, None)
    return jax.shard_map(
        on_device, mesh=mesh, in_specs=in_specs, out_specs=out_specs, check_vma=False
    )
```

time: 192 us -> 141 us (0.73)
  waiting for transfers between devices: 27.4 us -> 68.5 us
  starting transfers between devices: 88 us -> 50.1 us
  other arithmetic: 25.2 us -> 0 us
  blocking collectives: 25.1 us -> 0 us
  Pallas kernels: 0 us -> 18.4 us
  local copies, waits for them, and re-layouts: 13.6 us -> 2.24 us
  matrix products: 10.8 us -> 0 us
    ppermute x18 -> x23, waiting for transfers between devices: 9.38 us -> 68.5 us  [send(): return lax.ppermute(value, AXES, routes[route])]
    ppermute x18 -> x23, starting transfers between devices: 79.8 us -> 50.1 us  [send(): return lax.ppermute(value, AXES, routes[route])]
    all_to_all x1 -> x0, blocking collectives: 25.1 us -> none  [on_device(): lax.all_to_all(moved_state + update, 'inst', split_axis=0, concat_axis=3,...]
    pallas_call x0 -> x9, Pallas kernels: none -> 18.4 us  [call(): pl.pallas_call(kernel, name=name, out_shape=tuple((jax.ShapeDtypeStruct(s...]
    all_to_all x2 -> x0, waiting for transfers between devices: 18 us -> none  [the longest x1 18 us: on_device(): lax.all_to_all(local_part, 'inst', split_axis=3, concat_axis=0, tiled=True)]
    concatenate x5 -> x0, other arithmetic: 14.8 us -> none  [the longest x4 12.9 us: extended(): jnp.concatenate([jnp.pad(low, around), shard, jnp.pad(high, around)], axi...]
    dot_general x5 -> x0, matrix products: 10.8 us -> none  [spectral_term(): product = jnp.dot(matrix, flat, precision=lax.Precision.HIGHEST)]
    all_to_all x2 -> x0, starting transfers between devices: 8.12 us -> none  [the longest x1 4.42 us: on_device(): lax.all_to_all(local_part, 'inst', split_axis=3, concat_axis=0, tiled=True)]
  transfers between devices with their start and end apart: 20 -> 23, of which waited for: 6 -> 10; matrix products, arithmetic and copies ran while one was open for 6% -> 0% of each run, Pallas kernels for 0% -> 1%
where the time goes in v1:
time: 141 us; the launch traced here: 139 us
  waiting for transfers between devices  68.5 us (49%)
  starting transfers between devices  50.1 us (36%)
  Pallas kernels  18.4 us (13%)
  local copies, waits for them, and re-layouts  2.24 us (2%)
    ppermute x23, waiting for transfers between devices, send(): return lax.ppermute(value, AXES, routes[route])  68.5 us
    ppermute x23, starting transfers between devices, send(): return lax.ppermute(value, AXES, routes[route])  50.1 us
    pallas_call x9, Pallas kernels, call(): pl.pallas_call(kernel, name=name, out_shape=tuple((jax.ShapeDtypeStruct(s...  18.4 us
  transfers between devices with their start and end apart: 23, of which 10 were waited for; matrix products, arithmetic and copies ran while one was open for 0% of the time, Pallas kernels for 1%

profile of v1, /device:TPU:8, one launch (start us, length us, event | category | flops | bytes accessed | tf_op | source)
XLA Modules:
  0.0 139.5 jit_solution(11761184131164375530)
XLA Ops:
  0.0 1.3 copy-done
  1.3 1.0 state.1
  2.3 3.8 %collective-permute-start.3 = (f32[320,128]{1,0:T(8,128)S(1)}, f32[320,128]{1,0:T(8,128)S(1)}, u32[]{:S(2)}, u32[]{:S(2)}) collective-permute-start(f32[320,128]{1,0:T(8,128)S(1)} %get-tuple-element.35), channel_id=1, source_target_pairs={{0,1},{1,2},{2,3},{3,4},{4,5},{5,6},{6,7},{7,8},{8,9},{9,10},{10,1... | collective-permute-start | bytes 491528 | tf_op jit(solution)/shard_map/ppermute | solution.py:400
  6.2 7.9 %collective-permute-start.4 = (f32[320,128]{1,0:T(8,128)S(1)}, f32[320,128]{1,0:T(8,128)S(1)}, u32[]{:S(2)}, u32[]{:S(2)}) collective-permute-start(f32[320,128]{1,0:T(8,128)S(1)} %get-tuple-element.36), channel_id=1, source_target_pairs={{1,0},{2,1},{3,2},{4,3},{5,4},{6,5},{7,6},{8,7},{9,8},{10,9},{11,1... | collective-permute-start | bytes 491528 | tf_op jit(solution)/shard_map/ppermute | solution.py:400
  14.1 2.3 %collective-permute-done.3.lo = f32[320,128]{1,0:T(8,128)S(1)} collective-permute-done((f32[320,128]{1,0:T(8,128)S(1)}, f32[320,128]{1,0:T(8,128)S(1)}, u32[]{:S(2)}, u32[]{:S(2)}) %collective-permute-start.3) | collective-permute-done | bytes 163872 | tf_op jit(solution)/shard_map/ppermute | solution.py:400
  16.4 1.2 collective-permute-done.4.hi
  17.6 0.9 copy-done.4
  18.5 2.3 %part.1 = (f32[400,128]{1,0:T(8,128)S(1)}, f32[400,128]{1,0:T(8,128)S(1)}, f32[400,128]{1,0:T(8,128)S(1)}, f32[400,128]{1,0:T(8,128)S(1)}, f32[400,128]{1,0:T(8,...) custom-call(f32[2560,128]{1,0:T(8,128)S(1)} %bitcast.10, ...), custom_call_target="tpu_custom_call" | custom-call | tf_op jit(solution)/shard_map/part/pallas_call | solution.py:365
  20.8 0.1 collective-permute-start.5
  20.9 0.5 collective-permute-start.9
  21.4 0.1 collective-permute-start
  21.5 2.6 %collective-permute-start.1 = (f32[800,128]{1,0:T(8,128)S(1)}, f32[800,128]{1,0:T(8,128)S(1)}, u32[]{:S(2)}, u32[]{:S(2)}) collective-permute-start(f32[800,128]{1,0:T(8,128)S(1)} %get-tuple-element.33), channel_id=1, source_target_pairs={{0,128},{1,129},{2,130},{3,131},{4,132},{5,133},{6,134},{7,135},{8... | collective-permute-start | bytes 1228808 | tf_op jit(solution)/shard_map/ppermute | solution.py:400
  24.1 0.7 collective-permute-start.2
  24.8 0.0 collective-permute-done.5.refs_5_
  24.8 2.6 %collective-permute-start.10 = (f32[400,128]{1,0:T(8,128)S(1)}, f32[400,128]{1,0:T(8,128)S(1)}, u32[]{:S(2)}, u32[]{:S(2)}) collective-permute-start(f32[400,128]{1,0:T(8,128)S(1)} %get-tuple-element.43), channel_id=1, source_target_pairs={{0,128},{1,129},{2,130},{3,131},{4,132},{5,133},{6,134},{7,135},{8... | collective-permute-start | bytes 614408 | tf_op jit(solution)/shard_map/ppermute | solution.py:400
  27.3 0.0 collective-permute-done.9.refs_5_
  27.3 0.6 collective-permute-start.11
  28.0 0.4 inverse_pack.1
  28.4 20.1 %collective-permute-done.10.refs_6_ = f32[400,128]{1,0:T(8,128)S(1)} collective-permute-done((f32[400,128]{1,0:T(8,128)S(1)}, f32[400,128]{1,0:T(8,128)S(1)}, u32[]{:S(2)}, u32[]{:S(2)}) %collective-permute-start.10) | collective-permute-done | bytes 204832 | tf_op jit(solution)/shard_map/ppermute | solution.py:400
  48.5 3.3 %collective-permute-done.11.refs_7_ = f32[400,128]{1,0:T(8,128)S(1)} collective-permute-done((f32[400,128]{1,0:T(8,128)S(1)}, f32[400,128]{1,0:T(8,128)S(1)}, u32[]{:S(2)}, u32[]{:S(2)}) %collective-permute-start.11) | collective-permute-done | bytes 204832 | tf_op jit(solution)/shard_map/ppermute | solution.py:400
  51.8 2.6 %collective-permute-start.6 = (f32[400,128]{1,0:T(8,128)S(1)}, f32[400,128]{1,0:T(8,128)S(1)}, u32[]{:S(2)}, u32[]{:S(2)}) collective-permute-start(f32[400,128]{1,0:T(8,128)S(1)} %get-tuple-element.39), channel_id=1, source_target_pairs={{0,128},{1,129},{2,130},{3,131},{4,132},{5,133},{6,134},{7,135},{8... | collective-permute-start | bytes 614408 | tf_op jit(solution)/shard_map/ppermute | solution.py:400
  54.4 0.7 collective-permute-start.7
  55.0 0.0 collective-permute-done.1.refs_2_
  55.0 1.3 collective-permute-start.14
  56.3 0.7 collective-permute-start.15
  57.0 0.4 modes_inner.1
  57.4 3.8 %collective-permute-done.6.refs_6_ = f32[400,128]{1,0:T(8,128)S(1)} collective-permute-done((f32[400,128]{1,0:T(8,128)S(1)}, f32[400,128]{1,0:T(8,128)S(1)}, u32[]{:S(2)}, u32[]{:S(2)}) %collective-permute-start.6) | collective-permute-done | bytes 204832 | tf_op jit(solution)/shard_map/ppermute | solution.py:400
  61.2 1.8 %collective-permute-start.12 = (f32[1600,128]{1,0:T(8,128)S(1)}, f32[1600,128]{1,0:T(8,128)S(1)}, u32[]{:S(2)}, u32[]{:S(2)}) collective-permute-start(f32[1600,128]{1,0:T(8,128)S(1)} %modes_inner.1), channel_id=1, source_target_pairs={{0,64},{1,65},{2,66},{3,67},{4,68},{5,69},{6,70},{7,71},{8,72},{9,... | collective-permute-start | bytes 2457608 | tf_op jit(solution)/shard_map/ppermute | solution.py:400
  63.0 1.5 %collective-permute-done.7.refs_7_ = f32[400,128]{1,0:T(8,128)S(1)} collective-permute-done((f32[400,128]{1,0:T(8,128)S(1)}, f32[400,128]{1,0:T(8,128)S(1)}, u32[]{:S(2)}, u32[]{:S(2)}) %collective-permute-start.7) | collective-permute-done | bytes 204832 | tf_op jit(solution)/shard_map/ppermute | solution.py:400
  64.4 0.4 modes_edge.1
  64.8 8.6 %collective-permute-start.8 = (f32[1600,128]{1,0:T(8,128)S(1)}, f32[1600,128]{1,0:T(8,128)S(1)}, u32[]{:S(2)}, u32[]{:S(2)}) collective-permute-start(f32[1600,128]{1,0:T(8,128)S(1)} %modes_edge.1), channel_id=1, source_target_pairs={{1,64},{2,65},{3,66},{4,67},{5,68},{6,69},{7,70},{8,71},{9,72},{10... | collective-permute-start | bytes 2457608 | tf_op jit(solution)/shard_map/ppermute | solution.py:400
  73.4 0.0 collective-permute-done.14.halo2
  73.5 0.3 inverse_window.1
  73.8 4.0 %collective-permute-start.16 = (f32[1248,128]{1,0:T(8,128)S(1)}, f32[1248,128]{1,0:T(8,128)S(1)}, u32[]{:S(2)}, u32[]{:S(2)}) collective-permute-start(f32[1248,128]{1,0:T(8,128)S(1)} %get-tuple-element.49.be), channel_id=1, source_target_pairs={{1,64},{2,65},{3,66},{4,67},{5,68},{6,69},{7,70},{8,71},{9,72},{10... | collective-permute-start | bytes 1916936 | tf_op jit(solution)/shard_map/ppermute | solution.py:400
  77.8 0.1 collective-permute-start.17
  77.9 12.4 %collective-permute-done.16.bx = f32[1248,128]{1,0:T(8,128)S(1)} collective-permute-done((f32[1248,128]{1,0:T(8,128)S(1)}, f32[1248,128]{1,0:T(8,128)S(1)}, u32[]{:S(2)}, u32[]{:S(2)}) %collective-permute-start.16) | collective-permute-done | bytes 639008 | tf_op jit(solution)/shard_map/ppermute | solution.py:400
  90.3 6.8 %first.1 = (f32[180,8,128]{2,1,0:T(8,128)S(1)}, f32[180,8,128]{2,1,0:T(8,128)S(1)}) custom-call(f32[200,8,128]{2,1,0:T(8,128)S(1)} %bitcast.18, f32[200,8,128]{2,1,0:T(8,128)S(1)} %bitcast.14, f32[200,8,128]{2,1,0:T(8,128)S(1)} %bitcast.12, f32[200,8,128]{2,1,0:T(8,128)S(1)} %bitcast.16, f32[1248,128]{1,0:T(8,128)S(1)} %collective-permute-done.16.bx, ...), custom_call_target="tpu_custom_call" | custom-call | tf_op jit(solution)/shard_map/first/pallas_call | solution.py:365
  97.1 7.9 %collective-permute-start.18 = (f32[180,8,128]{2,1,0:T(8,128)S(1)}, f32[180,8,128]{2,1,0:T(8,128)S(1)}, u32[]{:S(2)}, u32[]{:S(2)}) collective-permute-start(f32[180,8,128]{2,1,0:T(8,128)S(1)} %get-tuple-element.51.ue), channel_id=1, source_target_pairs={{1,64},{2,65},{3,66},{4,67},{5,68},{6,69},{7,70},{8,71},{9,72},{10... | collective-permute-start | bytes 2211848 | tf_op jit(solution)/shard_map/ppermute | solution.py:400
  105.0 0.0 copy-start.1
  105.0 0.1 collective-permute-start.19
  105.1 9.1 %collective-permute-done.18.ux = f32[180,8,128]{2,1,0:T(8,128)S(1)} collective-permute-done((f32[180,8,128]{2,1,0:T(8,128)S(1)}, f32[180,8,128]{2,1,0:T(8,128)S(1)}, u32[]{:S(2)}, u32[]{:S(2)}) %collective-permute-start.18) | collective-permute-done | bytes 737312 | tf_op jit(solution)/shard_map/ppermute | solution.py:400
  114.2 5.5 %second.1 = (f32[640,128]{1,0:T(8,128)S(1)}, f32[640,128]{1,0:T(8,128)S(1)}, f32[640,128]{1,0:T(8,128)S(1)}, f32[640,128]{1,0:T(8,128)S(1)}) custom-call(f32[200,8,128]{2,1,0:T(8,128)S(1)} %bitcast.19, f32[200,8,128]{2,1,0:T(8,128)S(1)} %bitcast.15, f32[200,8,128]{2,1,0:T(8,128)S(1)} %bitcast.13, f32[200,8,128]{2,1,0:T(8,128)S(1)} %bitcast.17, ...), custom_call_target="tpu_custom_call" | custom-call | tf_op jit(solution)/shard_map/second/pallas_call | solution.py:365
  119.7 0.1 collective-permute-start.20
  119.8 3.5 %collective-permute-start.21 = (f32[640,128]{1,0:T(8,128)S(1)}, f32[640,128]{1,0:T(8,128)S(1)}, u32[]{:S(2)}, u32[]{:S(2)}) collective-permute-start(f32[640,128]{1,0:T(8,128)S(1)} %get-tuple-element.55), channel_id=1, source_target_pairs={{0,128},{1,129},{2,130},{3,131},{4,132},{5,133},{6,134},{7,135},{8... | collective-permute-start | bytes 983048 | tf_op jit(solution)/shard_map/ppermute | solution.py:400
  123.3 0.0 collective-permute-start.22
  123.3 8.7 %collective-permute-done.21.w2 = f32[640,128]{1,0:T(8,128)S(1)} collective-permute-done((f32[640,128]{1,0:T(8,128)S(1)}, f32[640,128]{1,0:T(8,128)S(1)}, u32[]{:S(2)}, u32[]{:S(2)}) %collective-permute-start.21) | collective-permute-done | bytes 327712 | tf_op jit(solution)/shard_map/ppermute | solution.py:400
  132.0 6.1 %collective-permute-done.22.w3 = f32[640,128]{1,0:T(8,128)S(1)} collective-permute-done((f32[640,128]{1,0:T(8,128)S(1)}, f32[640,128]{1,0:T(8,128)S(1)}, u32[]{:S(2)}, u32[]{:S(2)}) %collective-permute-start.22) | collective-permute-done | bytes 327712 | tf_op jit(solution)/shard_map/ppermute | solution.py:400
  138.2 1.3 final.1
  (19 shorter events, 0.0 us)
Async XLA Ops:
  0.0 1.3 copy-start
  1.3 16.2 %copy-start.2 = (f32[2,5,8,32,128]{4,3,2,1,0:T(8,128)S(1)}, f32[2,5,8,32,128]{4,3,2,1,0:T(8,128)}, u32[]{:S(2)}) copy-start(f32[2,5,8,32,128]{4,3,2,1,0:T(8,128)} %param.5) | copy-start | bytes 3932164
  2.3 14.0 %collective-permute-start.3 = (f32[320,128]{1,0:T(8,128)S(1)}, f32[320,128]{1,0:T(8,128)S(1)}, u32[]{:S(2)}, u32[]{:S(2)}) collective-permute-start(f32[320,128]{1,0:T(8,128)S(1)} %get-tuple-element.35), channel_id=1, source_target_pairs={{0,1},{1,2},{2,3},{3,4},{4,5},{5,6},{6,7},{7,8},{8,9},{9,10},{10,1... | collective-permute-start | bytes 491528 | tf_op jit(solution)/shard_map/ppermute | solution.py:400
  6.2 11.4 %collective-permute-start.4 = (f32[320,128]{1,0:T(8,128)S(1)}, f32[320,128]{1,0:T(8,128)S(1)}, u32[]{:S(2)}, u32[]{:S(2)}) collective-permute-start(f32[320,128]{1,0:T(8,128)S(1)} %get-tuple-element.36), channel_id=1, source_target_pairs={{1,0},{2,1},{3,2},{4,3},{5,4},{6,5},{7,6},{8,7},{9,8},{10,9},{11,1... | collective-permute-start | bytes 491528 | tf_op jit(solution)/shard_map/ppermute | solution.py:400
  17.5 0.9 copy-start.4
  18.5 9.5 %copy-start.3 = (f32[5,5,8,8,128]{4,3,2,1,0:T(8,128)S(1)}, f32[5,5,8,8,128]{4,3,2,1,0:T(8,128)}, u32[]{:S(2)}) copy-start(f32[5,5,8,8,128]{4,3,2,1,0:T(8,128)} %param.7) | copy-start | bytes 2457604
  20.8 4.0 %collective-permute-start.5 = (f32[400,128]{1,0:T(8,128)S(1)}, f32[400,128]{1,0:T(8,128)S(1)}, u32[]{:S(2)}, u32[]{:S(2)}) collective-permute-start(f32[400,128]{1,0:T(8,128)S(1)} %get-tuple-element.38), channel_id=1, source_target_pairs={{0,64},{1,65},{2,66},{3,67},{4,68},{5,69},{6,70},{7,71},{8,72},{9,... | collective-permute-start | bytes 614408 | tf_op jit(solution)/shard_map/ppermute | solution.py:400
  20.9 6.5 %collective-permute-start.9 = (f32[400,128]{1,0:T(8,128)S(1)}, f32[400,128]{1,0:T(8,128)S(1)}, u32[]{:S(2)}, u32[]{:S(2)}) collective-permute-start(f32[400,128]{1,0:T(8,128)S(1)} %get-tuple-element.42), channel_id=1, source_target_pairs={{0,64},{1,65},{2,66},{3,67},{4,68},{5,69},{6,70},{7,71},{8,72},{9,... | collective-permute-start | bytes 614408 | tf_op jit(solution)/shard_map/ppermute | solution.py:400
  21.4 33.0 %collective-permute-start = (f32[800,128]{1,0:T(8,128)S(1)}, f32[800,128]{1,0:T(8,128)S(1)}, u32[]{:S(2)}, u32[]{:S(2)}) collective-permute-start(f32[800,128]{1,0:T(8,128)S(1)} %get-tuple-element.32), channel_id=1, source_target_pairs={{0,64},{1,65},{2,66},{3,67},{4,68},{5,69},{6,70},{7,71},{8,72},{9,... | collective-permute-start | bytes 1228808 | tf_op jit(solution)/shard_map/ppermute | solution.py:400
  21.5 33.5 %collective-permute-start.1 = (f32[800,128]{1,0:T(8,128)S(1)}, f32[800,128]{1,0:T(8,128)S(1)}, u32[]{:S(2)}, u32[]{:S(2)}) collective-permute-start(f32[800,128]{1,0:T(8,128)S(1)} %get-tuple-element.33), channel_id=1, source_target_pairs={{0,128},{1,129},{2,130},{3,131},{4,132},{5,133},{6,134},{7,135},{8... | collective-permute-start | bytes 1228808 | tf_op jit(solution)/shard_map/ppermute | solution.py:400
  24.1 32.2 %collective-permute-start.2 = (f32[800,128]{1,0:T(8,128)S(1)}, f32[800,128]{1,0:T(8,128)S(1)}, u32[]{:S(2)}, u32[]{:S(2)}) collective-permute-start(f32[800,128]{1,0:T(8,128)S(1)} %get-tuple-element.34), channel_id=1, source_target_pairs={{0,192},{1,193},{2,194},{3,195},{4,196},{5,197},{6,198},{7,199},{8... | collective-permute-start | bytes 1228808 | tf_op jit(solution)/shard_map/ppermute | solution.py:400
  24.8 23.7 %collective-permute-start.10 = (f32[400,128]{1,0:T(8,128)S(1)}, f32[400,128]{1,0:T(8,128)S(1)}, u32[]{:S(2)}, u32[]{:S(2)}) collective-permute-start(f32[400,128]{1,0:T(8,128)S(1)} %get-tuple-element.43), channel_id=1, source_target_pairs={{0,128},{1,129},{2,130},{3,131},{4,132},{5,133},{6,134},{7,135},{8... | collective-permute-start | bytes 614408 | tf_op jit(solution)/shard_map/ppermute | solution.py:400
  27.3 24.4 %collective-permute-start.11 = (f32[400,128]{1,0:T(8,128)S(1)}, f32[400,128]{1,0:T(8,128)S(1)}, u32[]{:S(2)}, u32[]{:S(2)}) collective-permute-start(f32[400,128]{1,0:T(8,128)S(1)} %get-tuple-element.44), channel_id=1, source_target_pairs={{0,192},{1,193},{2,194},{3,195},{4,196},{5,197},{6,198},{7,199},{8... | collective-permute-start | bytes 614408 | tf_op jit(solution)/shard_map/ppermute | solution.py:400
  48.5 25.0 %collective-permute-start.13 = (f32[800,128]{1,0:T(8,128)S(1)}, f32[800,128]{1,0:T(8,128)S(1)}, u32[]{:S(2)}, u32[]{:S(2)}) collective-permute-start(f32[800,128]{1,0:T(8,128)S(1)} %get-tuple-element.46), channel_id=1, source_target_pairs={{0,64},{1,65},{2,66},{3,67},{4,68},{5,69},{6,70},{7,71},{8,72},{9,... | collective-permute-start | bytes 1228808 | tf_op jit(solution)/shard_map/ppermute | solution.py:400
  51.8 9.5 %collective-permute-start.6 = (f32[400,128]{1,0:T(8,128)S(1)}, f32[400,128]{1,0:T(8,128)S(1)}, u32[]{:S(2)}, u32[]{:S(2)}) collective-permute-start(f32[400,128]{1,0:T(8,128)S(1)} %get-tuple-element.39), channel_id=1, source_target_pairs={{0,128},{1,129},{2,130},{3,131},{4,132},{5,133},{6,134},{7,135},{8... | collective-permute-start | bytes 614408 | tf_op jit(solution)/shard_map/ppermute | solution.py:400
  54.4 10.1 %collective-permute-start.7 = (f32[400,128]{1,0:T(8,128)S(1)}, f32[400,128]{1,0:T(8,128)S(1)}, u32[]{:S(2)}, u32[]{:S(2)}) collective-permute-start(f32[400,128]{1,0:T(8,128)S(1)} %get-tuple-element.40), channel_id=1, source_target_pairs={{0,192},{1,193},{2,194},{3,195},{4,196},{5,197},{6,198},{7,199},{8... | collective-permute-start | bytes 614408 | tf_op jit(solution)/shard_map/ppermute | solution.py:400
  55.0 18.4 %collective-permute-start.14 = (f32[400,128]{1,0:T(8,128)S(1)}, f32[400,128]{1,0:T(8,128)S(1)}, u32[]{:S(2)}, u32[]{:S(2)}) collective-permute-start(f32[400,128]{1,0:T(8,128)S(1)} %get-tuple-element.47), channel_id=1, source_target_pairs={{64,192},{65,193},{66,194},{67,195},{68,196},{69,197},{70,198},{71... | collective-permute-start | bytes 614408 | tf_op jit(solution)/shard_map/ppermute | solution.py:400
  56.3 17.1 %collective-permute-start.15 = (f32[400,128]{1,0:T(8,128)S(1)}, f32[400,128]{1,0:T(8,128)S(1)}, u32[]{:S(2)}, u32[]{:S(2)}) collective-permute-start(f32[400,128]{1,0:T(8,128)S(1)} %get-tuple-element.48), channel_id=1, source_target_pairs={{64,128},{65,129},{66,130},{67,131},{68,132},{69,133},{70,134},{71... | collective-permute-start | bytes 614408 | tf_op jit(solution)/shard_map/ppermute | solution.py:400
  61.2 29.1 %collective-permute-start.12 = (f32[1600,128]{1,0:T(8,128)S(1)}, f32[1600,128]{1,0:T(8,128)S(1)}, u32[]{:S(2)}, u32[]{:S(2)}) collective-permute-start(f32[1600,128]{1,0:T(8,128)S(1)} %modes_inner.1), channel_id=1, source_target_pairs={{0,64},{1,65},{2,66},{3,67},{4,68},{5,69},{6,70},{7,71},{8,72},{9,... | collective-permute-start | bytes 2457608 | tf_op jit(solution)/shard_map/ppermute | solution.py:400
  64.4 9.0 %copy-start.5 = (f32[8,32,128]{2,1,0:T(8,128)S(1)}, f32[8,32,128]{2,1,0:T(8,128)}, u32[]{:S(2)}) copy-start(f32[8,32,128]{2,1,0:T(8,128)} %param.6) | copy-start | bytes 393220
  64.8 25.5 %collective-permute-start.8 = (f32[1600,128]{1,0:T(8,128)S(1)}, f32[1600,128]{1,0:T(8,128)S(1)}, u32[]{:S(2)}, u32[]{:S(2)}) collective-permute-start(f32[1600,128]{1,0:T(8,128)S(1)} %modes_edge.1), channel_id=1, source_target_pairs={{1,64},{2,65},{3,66},{4,67},{5,68},{6,69},{7,70},{8,71},{9,72},{10... | collective-permute-start | bytes 2457608 | tf_op jit(solution)/shard_map/ppermute | solution.py:400
  73.8 16.5 %collective-permute-start.16 = (f32[1248,128]{1,0:T(8,128)S(1)}, f32[1248,128]{1,0:T(8,128)S(1)}, u32[]{:S(2)}, u32[]{:S(2)}) collective-permute-start(f32[1248,128]{1,0:T(8,128)S(1)} %get-tuple-element.49.be), channel_id=1, source_target_pairs={{1,64},{2,65},{3,66},{4,67},{5,68},{6,69},{7,70},{8,71},{9,72},{10... | collective-permute-start | bytes 1916936 | tf_op jit(solution)/shard_map/ppermute | solution.py:400
  77.8 12.5 %collective-permute-start.17 = (f32[1248,128]{1,0:T(8,128)S(1)}, f32[1248,128]{1,0:T(8,128)S(1)}, u32[]{:S(2)}, u32[]{:S(2)}) collective-permute-start(f32[1248,128]{1,0:T(8,128)S(1)} %get-tuple-element.50.bi), channel_id=1, source_target_pairs={{0,64},{1,65},{2,66},{3,67},{4,68},{5,69},{6,70},{7,71},{8,72},{9,... | collective-permute-start | bytes 1916936 | tf_op jit(solution)/shard_map/ppermute | solution.py:400
  97.1 17.1 %collective-permute-start.18 = (f32[180,8,128]{2,1,0:T(8,128)S(1)}, f32[180,8,128]{2,1,0:T(8,128)S(1)}, u32[]{:S(2)}, u32[]{:S(2)}) collective-permute-start(f32[180,8,128]{2,1,0:T(8,128)S(1)} %get-tuple-element.51.ue), channel_id=1, source_target_pairs={{1,64},{2,65},{3,66},{4,67},{5,68},{6,69},{7,70},{8,71},{9,72},{10... | collective-permute-start | bytes 2211848 | tf_op jit(solution)/shard_map/ppermute | solution.py:400
  105.0 33.1 %copy-start.1 = (f32[2,5,8,32,128]{4,3,2,1,0:T(8,128)S(1)}, f32[2,5,8,32,128]{4,3,2,1,0:T(8,128)}, u32[]{:S(2)}) copy-start(f32[2,5,8,32,128]{4,3,2,1,0:T(8,128)} %param.4) | copy-start | bytes 3932164
  105.0 9.2 %collective-permute-start.19 = (f32[180,8,128]{2,1,0:T(8,128)S(1)}, f32[180,8,128]{2,1,0:T(8,128)S(1)}, u32[]{:S(2)}, u32[]{:S(2)}) collective-permute-start(f32[180,8,128]{2,1,0:T(8,128)S(1)} %get-tuple-element.52.ui), channel_id=1, source_target_pairs={{0,64},{1,65},{2,66},{3,67},{4,68},{5,69},{6,70},{7,71},{8,72},{9,... | collective-permute-start | bytes 2211848 | tf_op jit(solution)/shard_map/ppermute | solution.py:400
  119.7 3.6 %collective-permute-start.20 = (f32[640,128]{1,0:T(8,128)S(1)}, f32[640,128]{1,0:T(8,128)S(1)}, u32[]{:S(2)}, u32[]{:S(2)}) collective-permute-start(f32[640,128]{1,0:T(8,128)S(1)} %get-tuple-element.54), channel_id=1, source_target_pairs={{0,64},{1,65},{2,66},{3,67},{4,68},{5,69},{6,70},{7,71},{8,72},{9,... | collective-permute-start | bytes 983048 | tf_op jit(solution)/shard_map/ppermute | solution.py:400
  119.8 12.2 %collective-permute-start.21 = (f32[640,128]{1,0:T(8,128)S(1)}, f32[640,128]{1,0:T(8,128)S(1)}, u32[]{:S(2)}, u32[]{:S(2)}) collective-permute-start(f32[640,128]{1,0:T(8,128)S(1)} %get-tuple-element.55), channel_id=1, source_target_pairs={{0,128},{1,129},{2,130},{3,131},{4,132},{5,133},{6,134},{7,135},{8... | collective-permute-start | bytes 983048 | tf_op jit(solution)/shard_map/ppermute | solution.py:400
  123.3 14.9 %collective-permute-start.22 = (f32[640,128]{1,0:T(8,128)S(1)}, f32[640,128]{1,0:T(8,128)S(1)}, u32[]{:S(2)}, u32[]{:S(2)}) collective-permute-start(f32[640,128]{1,0:T(8,128)S(1)} %get-tuple-element.56), channel_id=1, source_target_pairs={{0,192},{1,193},{2,194},{3,195},{4,196},{5,197},{6,198},{7,199},{8... | collective-permute-start | bytes 983048 | tf_op jit(solution)/shard_map/ppermute | solution.py:400
